TPU v7x, 32 devices: a whole 2x2x4 slice. The times are simulated.
32 devices in a mesh: seq: 8 (over z, y), head: 4 (over x, core).
Axes of the slice: x: 2, y: 2, z: 4, core: 2. Of those that a mesh axis runs over, the one named last changes fastest.
Arguments:
- queries: bfloat16 [2048, 4096], P('seq', 'head'), may hold values from -8 to 8
- self_keys: bfloat16 [2048, 1024], P('seq', 'head'), may hold values from -6 to 6
- self_values: bfloat16 [2048, 1024], P('seq', 'head'), may hold values from -6 to 6
- store_keys: bfloat16 [32768, 1024], P('seq', 'head'), may hold values from -6 to 6
- store_values: bfloat16 [32768, 1024], P('seq', 'head'), may hold values from -6 to 6
- kv_slot: int32 [256], replicated, may hold values from 0 to 255, as said below
- neighbours: int32 [16, 64], P('seq'), may hold values from 0 to 255, as said below
- counts: int32 [16], P('seq'), may hold values from 1 to 64, 96 in all
- out_weight: bfloat16 [4096, 4096], P('head', 'seq'), may hold values from -0.375 to 0.375
Outputs:
- mixed: bfloat16 [2048, 4096], P(('seq', 'head'))
Inputs may be any that keep to these rules, and one draw needn't show every extreme that they name: A permutation of the store blocks: block b is stored at slot kv_slot[b], on index kv_slot[b] // 32 of seq. `neighbours`: each row names 64 different store blocks in no particular order; only entries e < counts of the row are listed, the rest is padding. Counting by the index of seq on which a block is stored, each row names exactly 8 blocks on every index, and the 2 rows of one index of seq name the same single block on every index of seq.
All inputs are finite; a program needn't handle non-finite values. No bound on the sum of `counts` on one device may be relied on, other than what follows from the above.
Results may differ from a plain program's by a relative error of at most 0.012.
Values may be sent and summed in bfloat16 or wider, within the bound.
A program may use at most 128 MiB of HBM per device.

v0:
```python
import functools

import jax
import jax.numpy as jnp
from jax import lax
from jax.experimental import pallas as pl
from jax.experimental.pallas import tpu as pltpu
from jax.sharding import PartitionSpec as P

H = 32
KVH = 8
DH = 128
BLK = 128
NEG = -1e30
STAT = 8
MESH = pl.DeviceIdType.MESH


def part_kernel(
    local_blocks,
    store_blocks,
    slot_ref,
    near_ref,
    count_ref,
    q_ref,
    sk_ref,
    sv_ref,
    k_ref,
    v_ref,
    o_ref,
    lse_ref,
    list_ref,
    acc_ref,
    max_ref,
    sum_ref,
):
    block = pl.program_id(0)
    me = lax.axis_index("seq")
    per_group = H // KVH
    kv_here = k_ref.shape[1] // DH
    rows = per_group * BLK
    scaling = DH ** (-0.5)

    def scan_entry(e, found):
        slot = slot_ref[near_ref[block, e]]
        list_ref[found] = lax.rem(slot, store_blocks)
        return found + (slot // store_blocks == me).astype(jnp.int32)

    found = lax.fori_loop(0, count_ref[block], scan_entry, jnp.int32(0))
    home = block // local_blocks == me

    @pl.when(jnp.logical_and(found == 0, jnp.logical_not(home)))
    def _():
        o_ref[...] = jnp.zeros_like(o_ref)
        lse_ref[...] = jnp.full_like(lse_ref, NEG)

    @pl.when(jnp.logical_or(found > 0, home))
    def _():
        def group_queries(g):
            return jnp.concatenate(
                [q_ref[:, (g * per_group + r) * DH : (g * per_group + r + 1) * DH] for r in range(per_group)],
                axis=0,
            )

        def scores_of(g, keys):
            return (
                lax.dot_general(
                    group_queries(g), keys, (((1,), (1,)), ((), ())), preferred_element_type=jnp.float32
                )
                * scaling
            )

        @pl.when(home)
        def _():
            start = pl.multiple_of(lax.rem(block, local_blocks) * BLK, BLK)
            position = lax.rem(lax.broadcasted_iota(jnp.int32, (rows, BLK), 0), BLK)
            causal = position >= lax.broadcasted_iota(jnp.int32, (rows, BLK), 1)
            for g in range(kv_here):
                cols = slice(g * DH, (g + 1) * DH)
                s = jnp.where(causal, scores_of(g, sk_ref[pl.ds(start, BLK), cols]), NEG)
                m = jnp.max(s, axis=-1, keepdims=True)
                p = jnp.exp(s - m)
                max_ref[g] = jnp.broadcast_to(m, (rows, BLK))
                sum_ref[g] = jnp.broadcast_to(jnp.sum(p, axis=-1, keepdims=True), (rows, BLK))
                acc_ref[g] = jnp.dot(
                    p.astype(jnp.bfloat16), sv_ref[pl.ds(start, BLK), cols], preferred_element_type=jnp.float32
                )

        @pl.when(jnp.logical_not(home))
        def _():
            max_ref[...] = jnp.full_like(max_ref, NEG)
            sum_ref[...] = jnp.zeros_like(sum_ref)
            acc_ref[...] = jnp.zeros_like(acc_ref)

        @pl.loop(0, found)
        def _(i):
            start = pl.multiple_of(list_ref[i] * BLK, BLK)
            for g in range(kv_here):
                cols = slice(g * DH, (g + 1) * DH)
                s = scores_of(g, k_ref[pl.ds(start, BLK), cols])
                old = max_ref[g]
                new = jnp.maximum(old, jnp.max(s, axis=-1, keepdims=True))
                p = jnp.exp(s - new)
                shrink = jnp.exp(old - new)
                max_ref[g] = new
                sum_ref[g] = sum_ref[g] * shrink + jnp.sum(p, axis=-1, keepdims=True)
                acc_ref[g] = acc_ref[g] * shrink + jnp.dot(
                    p.astype(jnp.bfloat16), v_ref[pl.ds(start, BLK), cols], preferred_element_type=jnp.float32
                )

        lane = lax.broadcasted_iota(jnp.int32, (BLK, BLK), 1)
        for g in range(kv_here):
            total = sum_ref[g]
            normal = (acc_ref[g] / total).astype(jnp.bfloat16)
            lse = max_ref[g] + jnp.log(total)
            tile = jnp.full((BLK, BLK), NEG, jnp.float32)
            for r in range(per_group):
                o_ref[0, g, :, r * DH : (r + 1) * DH] = normal[r * BLK : (r + 1) * BLK]
                tile = jnp.where(lane == r, lse[r * BLK : (r + 1) * BLK], tile)
            lse_ref[0, g] = jnp.transpose(tile)[:STAT]


def ring_place(index, n):
    odd = lax.rem(index, 2)
    half = index // 2
    return (1 - odd) * half + odd * (n - 1 - half)


def ring_index(place, n):
    place = lax.rem(place + 2 * n, n)
    far = place // (n // 2)
    return (1 - far) * (2 * place) + far * (2 * (n - 1 - place) + 1)


def gather_kernel(n, pieces, with_table, *refs):
    if with_table:
        x_ref, table_ref, out_ref, tables_ref, own_sem, send_sem, recv_sem, tsend_sem, trecv_sem = refs
    else:
        x_ref, out_ref, own_sem, send_sem, recv_sem = refs
    me = lax.axis_index("seq")
    place = ring_place(me, n)
    rows = x_ref.shape[0]
    sub = rows // pieces
    half = n // 2
    ways = (1, -1)
    beside = [ring_index(place + way, n) for way in ways]
    barrier = pltpu.get_barrier_semaphore()
    if with_table:
        for k in range(1, n):
            pl.semaphore_signal(barrier, inc=1, device_id={"seq": lax.rem(me + k, n)}, device_id_type=MESH)
    else:
        for other in beside:
            pl.semaphore_signal(barrier, inc=1, device_id={"seq": other}, device_id_type=MESH)
    own = pltpu.make_async_copy(x_ref, out_ref.at[pl.ds(pl.multiple_of(me * rows, rows), rows)], own_sem.at[0])
    own.start()
    pl.semaphore_wait(barrier, n - 1 if with_table else 2)

    def copy(way, step, piece):
        owner = ring_index(place - ways[way] * step, n)
        there = pl.ds(pl.multiple_of(owner * rows + piece * sub, sub), sub)
        source = x_ref.at[pl.ds(piece * sub, sub)] if step == 0 else out_ref.at[there]
        return pltpu.make_async_remote_copy(
            src_ref=source,
            dst_ref=out_ref.at[there],
            send_sem=send_sem.at[way, step, piece],
            recv_sem=recv_sem.at[way, step, piece],
            device_id={"seq": beside[way]},
            device_id_type=MESH,
        )

    table_copies = []
    if with_table:
        tables_ref[pl.ds(me, 1)] = table_ref[...][None]
        for k in range(1, n):
            table_copies.append(
                pltpu.make_async_remote_copy(
                    src_ref=table_ref,
                    dst_ref=tables_ref.at[me],
                    send_sem=tsend_sem.at[k],
                    recv_sem=trecv_sem.at[k],
                    device_id={"seq": lax.rem(me + k, n)},
                    device_id_type=MESH,
                )
            )
        for one in table_copies:
            one.start()
    started = []
    for step in range(half):
        for spot in range(pieces):
            for way in range(2):
                piece = spot if way == 0 else pieces - 1 - spot
                if step > 0:
                    copy(way, step - 1, piece).wait_recv()
                if step < half - 1 or spot < pieces // 2:
                    one = copy(way, step, piece)
                    one.start()
                    started.append(one)
    for spot in range(pieces // 2):
        for way in range(2):
            copy(way, half - 1, spot if way == 0 else pieces - 1 - spot).wait_recv()
    for one in started:
        one.wait_send()
    for one in table_copies:
        one.wait()
    own.wait()


def gathered(x, n, pieces, number, table=None):
    rows, width = x.shape
    with_table = table is not None
    vmem = pl.BlockSpec(memory_space=pltpu.VMEM)
    out_shape = [jax.ShapeDtypeStruct((n * rows, width), x.dtype)]
    scratch = [
        pltpu.SemaphoreType.DMA((1,)),
        pltpu.SemaphoreType.DMA((2, n // 2, pieces)),
        pltpu.SemaphoreType.DMA((2, n // 2, pieces)),
    ]
    if with_table:
        out_shape.append(jax.ShapeDtypeStruct((n,) + table.shape, table.dtype))
        scratch += [pltpu.SemaphoreType.DMA((n,)), pltpu.SemaphoreType.DMA((n,))]
    return pl.pallas_call(
        functools.partial(gather_kernel, n, pieces, with_table),
        in_specs=[vmem] * (1 + with_table),
        out_specs=[vmem] * (1 + with_table),
        out_shape=out_shape,
        scratch_shapes=scratch,
        compiler_params=pltpu.CompilerParams(
            collective_id=number, has_side_effects=True, vmem_limit_bytes=50 << 20
        ),
    )(*([x, table] if with_table else [x]))


def merge(lse_a, lse_b):
    top = jnp.maximum(lse_a, lse_b)
    a = jnp.exp(lse_a - top)
    b = jnp.exp(lse_b - top)
    total = a + b
    both = jnp.concatenate([a / total, b / total, jnp.zeros((BLK - 2 * STAT, BLK), jnp.float32)], axis=0)
    return jnp.transpose(both), top + jnp.log(total)


def reduce_kernel(n, o_ref, lse_ref, out_ref, got, got_lse, own, own_sem, send_sem, recv_sem, lsend_sem, lrecv_sem):
    me = lax.axis_index("seq")
    place = ring_place(me, n)
    groups, width = got.shape[2], got.shape[4]
    ways = (1, -1)
    beside = [ring_index(place + way, n) for way in ways]
    barrier = pltpu.get_barrier_semaphore()
    for other in beside:
        pl.semaphore_signal(barrier, inc=1, device_id={"seq": other}, device_id_type=MESH)

    def home(way, step):
        return ring_index(place - ways[way] * (1 + step), n)

    def fetch(way, step):
        return pltpu.make_async_copy(
            o_ref.at[home(way, step) * 2 + way], own.at[way, lax.rem(step, 2)], own_sem.at[way, lax.rem(step, 2)]
        )

    def copies(way, step, g, before):
        at = home(way, step) * 2 + way
        first = before is None
        return (
            pltpu.make_async_remote_copy(
                src_ref=lse_ref.at[at, g] if first else got_lse.at[way, before, g],
                dst_ref=got_lse.at[way, step, g],
                send_sem=lsend_sem.at[way, step, g],
                recv_sem=lrecv_sem.at[way, step, g],
                device_id={"seq": beside[way]},
                device_id_type=MESH,
            ),
            pltpu.make_async_remote_copy(
                src_ref=o_ref.at[at, g] if first else got.at[way, before, g],
                dst_ref=got.at[way, step, g],
                send_sem=send_sem.at[way, step, g],
                recv_sem=recv_sem.at[way, step, g],
                device_id={"seq": beside[way]},
                device_id_type=MESH,
            ),
        )

    def merged(way, step, g):
        for one in copies(way, step - 1, g, step - 1):
            one.wait_recv()
        if g == 0:
            fetch(way, step).wait()
        at = home(way, step) * 2 + way
        shares, lse = merge(got_lse[way, step - 1, g], lse_ref[at, g])
        columns = []
        for r in range(width // DH):
            cols = slice(r * DH, (r + 1) * DH)
            columns.append(
                got[way, step - 1, g, :, cols].astype(jnp.float32) * shares[:, r : r + 1]
                + own[way, lax.rem(step, 2), g, :, cols].astype(jnp.float32) * shares[:, STAT + r : STAT + r + 1]
            )
        return columns, lse

    for way in range(2):
        fetch(way, 1).start()
    pl.semaphore_wait(barrier, 2)
    for g in range(groups):
        for way in range(2):
            for one in copies(way, 0, g, None):
                one.start()

    def one_step(step, carry):
        for way in range(2):
            fetch(way, step + 1).start()
        for g in range(groups):
            for way in range(2):
                columns, lse = merged(way, step, g)
                got_lse[way, step - 1, g] = lse
                for r, value in enumerate(columns):
                    got[way, step - 1, g, :, r * DH : (r + 1) * DH] = value.astype(jnp.bfloat16)
            for way in range(2):
                for one in copies(way, step, g, step - 1):
                    one.start()
        return carry

    lax.fori_loop(1, n - 1, one_step, 0)
    for g in range(groups):
        for way in range(2):
            columns, _ = merged(way, n - 1, g)
            for r, value in enumerate(columns):
                at = g * width + r * DH
                out_ref[way * BLK : (way + 1) * BLK, at : at + DH] = value.astype(jnp.bfloat16)
    for g in range(groups):
        for way in range(2):
            for one in copies(way, 0, g, None):
                one.wait_send()

    def drain(step, carry):
        for g in range(groups):
            for way in range(2):
                for one in copies(way, step, g, step - 1):
                    one.wait_send()
        return carry

    lax.fori_loop(1, n - 1, drain, 0)


def finish_kernel(n, heads, p_ref, out_ref, got, summed, landed, hsend, hrecv, send_sem, recv_sem):
    me = lax.axis_index("seq")
    mine = lax.axis_index("head")
    columns = p_ref.shape[3]
    barrier = pltpu.get_barrier_semaphore()
    for k in range(1, heads):
        pl.semaphore_signal(barrier, inc=1, device_id={"head": lax.rem(mine + k, heads)}, device_id_type=MESH)
    for k in range(1, n):
        pl.semaphore_signal(barrier, inc=1, device_id={"seq": lax.rem(me + k, n)}, device_id_type=MESH)
    pl.semaphore_wait(barrier, heads + n - 2)
    first = []
    for k in range(1, heads):
        to = lax.rem(mine + k, heads)
        first.append(
            pltpu.make_async_remote_copy(
                src_ref=p_ref.at[to],
                dst_ref=got.at[k],
                send_sem=hsend.at[k],
                recv_sem=hrecv.at[k],
                device_id={"head": to},
                device_id_type=MESH,
            )
        )
    for one in first:
        one.start()
    for one in first:
        one.wait()

    def add(i, carry):
        total = p_ref[mine, i].astype(jnp.float32)
        for k in range(1, heads):
            total = total + got[k, i].astype(jnp.float32)
        summed[i] = total.astype(jnp.bfloat16)
        return carry

    lax.fori_loop(0, n, add, 0)
    second = []
    for k in range(1, n):
        to = lax.rem(me + k, n)
        second.append(
            pltpu.make_async_remote_copy(
                src_ref=summed.at[to],
                dst_ref=landed.at[me],
                send_sem=send_sem.at[k],
                recv_sem=recv_sem.at[k],
                device_id={"seq": to},
                device_id_type=MESH,
            )
        )
    for one in second:
        one.start()
    landed[me] = summed[me]
    for one in second:
        one.wait()
    for i in range(n):
        out_ref[:, i * columns : (i + 1) * columns] = landed[i]


def finished(split):
    heads, n, share, columns = split.shape
    vmem = pl.BlockSpec(memory_space=pltpu.VMEM)
    return pl.pallas_call(
        functools.partial(finish_kernel, n, heads),
        in_specs=[vmem],
        out_specs=vmem,
        out_shape=jax.ShapeDtypeStruct((share, n * columns), split.dtype),
        scratch_shapes=[
            pltpu.VMEM(split.shape, split.dtype),
            pltpu.VMEM((n, share, columns), split.dtype),
            pltpu.VMEM((n, share, columns), split.dtype),
            pltpu.SemaphoreType.DMA((heads,)),
            pltpu.SemaphoreType.DMA((heads,)),
            pltpu.SemaphoreType.DMA((n,)),
            pltpu.SemaphoreType.DMA((n,)),
        ],
        compiler_params=pltpu.CompilerParams(
            collective_id=3, has_side_effects=True, vmem_limit_bytes=50 << 20
        ),
    )(split)


def body(
    queries,
    self_keys,
    self_values,
    store_keys,
    store_values,
    kv_slot,
    neighbours,
    counts,
    out_weight,
):
    n = lax.axis_size("seq")
    head_count = lax.axis_size("head")
    local_blocks, degree = neighbours.shape
    local_rows, width = queries.shape
    store_blocks = store_keys.shape[0] // BLK
    all_blocks = local_blocks * n
    kv_here = store_keys.shape[1] // DH
    group_width = (H // KVH) * DH
    rows = (H // KVH) * BLK
    table = jnp.concatenate([neighbours, counts[:, None]], axis=1)
    table = jnp.pad(table, ((0, 8 - local_blocks), (0, 2 * BLK - table.shape[1] - BLK)))
    all_queries, tables = gathered(queries, n, 2, 0, table)
    near = tables[:, :local_blocks, :degree].reshape(all_blocks, degree)
    count = tables[:, :local_blocks, degree].reshape(all_blocks)
    smem = pl.BlockSpec(memory_space=pltpu.SMEM)

    def whole(a):
        return pl.BlockSpec(a.shape, lambda i: (0, 0))

    parts, lse = pl.pallas_call(
        functools.partial(part_kernel, local_blocks, store_blocks),
        grid=(all_blocks,),
        in_specs=[smem, smem, smem, pl.BlockSpec((BLK, width), lambda i: (i, 0))]
        + [whole(a) for a in (self_keys, self_values, store_keys, store_values)],
        out_specs=[
            pl.BlockSpec((1, kv_here, BLK, group_width), lambda i: (i, 0, 0, 0)),
            pl.BlockSpec((1, kv_here, STAT, BLK), lambda i: (i, 0, 0, 0)),
        ],
        out_shape=[
            jax.ShapeDtypeStruct((all_blocks, kv_here, BLK, group_width), jnp.bfloat16),
            jax.ShapeDtypeStruct((all_blocks, kv_here, STAT, BLK), jnp.float32),
        ],
        scratch_shapes=[
            pltpu.SMEM((degree + 1,), jnp.int32),
            pltpu.VMEM((kv_here, rows, DH), jnp.float32),
            pltpu.VMEM((kv_here, rows, BLK), jnp.float32),
            pltpu.VMEM((kv_here, rows, BLK), jnp.float32),
        ],
        compiler_params=pltpu.CompilerParams(vmem_limit_bytes=40 << 20),
        cost_estimate=pl.CostEstimate(flops=2_000_000_000, bytes_accessed=12 << 20, transcendentals=4_000_000),
    )(kv_slot, near, count, all_queries, self_keys, self_values, store_keys, store_values)
    dma = pltpu.SemaphoreType.DMA((2, n - 1, kv_here))
    attended = pl.pallas_call(
        functools.partial(reduce_kernel, n),
        in_specs=[pl.BlockSpec(memory_space=pl.ANY), pl.BlockSpec(memory_space=pltpu.VMEM)],
        out_specs=pl.BlockSpec(memory_space=pltpu.VMEM),
        out_shape=jax.ShapeDtypeStruct((local_rows, width), jnp.bfloat16),
        scratch_shapes=[
            pltpu.VMEM((2, n - 1, kv_here, BLK, group_width), jnp.bfloat16),
            pltpu.VMEM((2, n - 1, kv_here, STAT, BLK), jnp.float32),
            pltpu.VMEM((2, 2, kv_here, BLK, group_width), jnp.bfloat16),
            pltpu.SemaphoreType.DMA((2, 2)),
            dma,
            dma,
            dma,
            dma,
        ],
        compiler_params=pltpu.CompilerParams(
            collective_id=1, has_side_effects=True, vmem_limit_bytes=50 << 20
        ),
    )(parts, lse)
    (all_attended,) = gathered(attended, n, 2, 2)
    partial_value = jnp.dot(all_attended, out_weight, preferred_element_type=jnp.float32).astype(jnp.bfloat16)
    columns = out_weight.shape[1]
    share = local_rows // head_count
    split = partial_value.reshape(n, head_count, share, columns).transpose(1, 0, 2, 3)
    return finished(split)


def solution(mesh):
    placed = (
        P("seq", "head"),
        P("seq", "head"),
        P("seq", "head"),
        P("seq", "head"),
        P("seq", "head"),
        P(),
        P("seq", None),
        P("seq"),
        P("head", "seq"),
    )
    return jax.shard_map(
        body, mesh=mesh, in_specs=placed, out_specs=P(("seq", "head"), None), check_vma=False
    )
```

profile of v0, /device:TPU:13, one launch (start us, length us, event | category | flops | bytes accessed | tf_op | source)
XLA Modules:
  0.0 207.0 jit_solution(15536063896964228319)
XLA Ops:
  0.0 0.0 copy-start
  0.0 0.8 copy.11
  0.8 0.8 pad_add_fusion
  1.6 0.0 copy-start.5
  1.6 1.0 copy-done.5
  2.6 45.9 %shard_map.91 = (bf16[2048,1024]{1,0:T(8,128)(2,1)}, s32[8,8,128]{2,1,0:T(8,128)S(1)}) custom-call(bf16[256,1024]{1,0:T(8,128)(2,1)S(1)} %copy-done.5, s32[8,128]{1,0:T(8,128)S(1)} %pad.4.refs_1_), custom_call_target="tpu_custom_call" | custom-call | tf_op jit(solution)/shard_map/pallas_call | solution.py:221
  48.5 0.3 slice_reduce_fusion
  48.8 0.1 reshape_squeeze.3.count_ref
  48.9 0.0 copy-start.2
  48.9 2.2 %copy-done.2 = bf16[2048,1024]{1,0:T(8,128)(2,1)S(1)} copy-done((bf16[2048,1024]{1,0:T(8,128)(2,1)S(1)}, bf16[2048,1024]{1,0:T(8,128)(2,1)}, u32[]{:S(2)}) %copy-start.2) | copy-done | bytes 4194328
  51.1 0.0 copy-start.3
  51.1 1.6 copy-done.3
  52.7 0.0 copy-start.4
  52.7 1.6 copy-done.4
  54.3 0.0 copy-start.6
  54.3 0.9 copy-done.6
  55.2 0.0 copy-start.7
  55.2 0.9 copy-done.7
  56.1 0.0 copy-start.8
  56.1 0.7 copy-done.8
  56.7 15.9 %shard_map.92 = (bf16[16,2,128,512]{3,2,1,0:T(8,128)(2,1)S(1)}, f32[16,2,8,128]{3,2,1,0:T(8,128)S(1)}) custom-call(s32[256]{0:T(256)S(1)} %copy-done.8, s32[16,64]{1,0:T(8,128)S(1)} %bitcast.9, s32[16]{0:T(128)S(1)} %reshape_squeeze.3.count_ref, bf16[2048,1024]{1,0:T(8,128)(2,1)S(1)} %copy-done.2, bf16[256,256]{1,0:T(8,128)(2,1)S(1)} %copy-done.6, ...), custom_call_target="tpu_custom_call" | custom-call | flops 2000000000 | bytes 12582912 | tf_op jit(solution)/shard_map/pallas_call | solution.py:453
  72.7 0.0 copy-start.1
  72.7 1.9 copy-done.1
  74.6 43.3 %shard_map.93.refs_0_ = bf16[256,1024]{1,0:T(8,128)(2,1)S(1)} custom-call(bf16[16,2,128,512]{3,2,1,0:T(8,128)(2,1)} %copy-done.1, f32[16,2,8,128]{3,2,1,0:T(8,128)S(1)} %get-tuple-element.12.lse_ref), custom_call_target="tpu_custom_call" | custom-call | tf_op jit(solution)/shard_map/pallas_call | solution.py:476
  117.9 41.5 %shard_map.94 = bf16[2048,1024]{1,0:T(8,128)(2,1)} custom-call(bf16[256,1024]{1,0:T(8,128)(2,1)S(1)} %shard_map.93.refs_0_), custom_call_target="tpu_custom_call" | custom-call | tf_op jit(solution)/shard_map/pallas_call | solution.py:221
  159.4 0.0 copy-done
  159.4 4.5 %convolution_convert_fusion = bf16[2048,512]{1,0:T(8,128)(2,1)S(1)} fusion(bf16[2048,1024]{1,0:T(8,128)(2,1)} %shard_map.94, bf16[1024,512]{1,0:T(8,128)(2,1)S(1)} %copy-done), kind=kOutput, calls=%fused_computation | convolution fusion | flops 2148532224 | bytes 7340032 | tf_op jit(solution)/shard_map/dot_general | solution.py:496
  164.0 0.1 copy.14
  164.1 42.1 %shard_map.95 = bf16[64,4096]{1,0:T(8,128)(2,1)S(1)} custom-call(bf16[4,8,64,512]{3,2,1,0:T(8,128)(2,1)S(1)} %bitcast.8), custom_call_target="tpu_custom_call" | custom-call | tf_op jit(solution)/shard_map/pallas_call | solution.py:403
  206.2 0.8 copy.16
  (2 shorter events, 0.0 us)
Async XLA Ops:
  0.0 159.4 %copy-start = (bf16[1024,512]{1,0:T(8,128)(2,1)S(1)}, bf16[1024,512]{1,0:T(8,128)(2,1)}, u32[]{:S(2)}) copy-start(bf16[1024,512]{1,0:T(8,128)(2,1)} %param.17) | copy-start | bytes 3145732
  1.6 1.0 copy-start.5
  48.9 2.2 %copy-start.2 = (bf16[2048,1024]{1,0:T(8,128)(2,1)S(1)}, bf16[2048,1024]{1,0:T(8,128)(2,1)}, u32[]{:S(2)}) copy-start(bf16[2048,1024]{1,0:T(8,128)(2,1)} %get-tuple-element.10.q_ref) | copy-start | bytes 12582916
  51.1 1.6 copy-start.3
  52.7 1.6 copy-start.4
  54.3 0.9 copy-start.6
  55.2 0.9 copy-start.7
  56.1 0.7 copy-start.8
  72.7 1.9 copy-start.1
where the time goes:
time: 208 us; the launch traced here: 207 us
  Pallas kernels  189 us (91%)
  local copies, waits for them, and re-layouts  13 us (6%)
  matrix products  4.52 us (2%)
    pallas_call x2, Pallas kernels, gathered(): pl.pallas_call(functools.partial(gather_kernel, n, pieces, with_table), i...  87.4 us
    pallas_call x1, Pallas kernels, body(): pl.pallas_call(functools.partial(reduce_kernel, n), in_specs=[pl.BlockSpe...  43.3 us
    pallas_call x1, Pallas kernels, finished(): pl.pallas_call(functools.partial(finish_kernel, n, heads), in_specs=[vmem...  42.1 us
    pallas_call x1, Pallas kernels, body(): pl.pallas_call(functools.partial(part_kernel, local_blocks, store_blocks)...  15.9 us
    unnamed x19, local copies, waits for them, and re-layouts  11.6 us
    dot_general x1, matrix products, body(): jnp.dot(all_attended, out_weight, preferred_element_type=jnp.float32)  4.52 us

commit v1 on v0

--- a/solution.py
+++ b/solution.py
@@ -339,85 +339,204 @@
     lax.fori_loop(1, n - 1, drain, 0)
 
 
-def finish_kernel(n, heads, p_ref, out_ref, got, summed, landed, hsend, hrecv, send_sem, recv_sem):
+def project_kernel(
+    n,
+    heads,
+    pieces,
+    x_ref,
+    w_hbm,
+    out_ref,
+    w_ref,
+    blocks,
+    split,
+    got,
+    summed,
+    landed,
+    w_sem,
+    send_sem,
+    recv_sem,
+    hsend,
+    hrecv,
+    fsend,
+    frecv,
+):
     me = lax.axis_index("seq")
     mine = lax.axis_index("head")
-    columns = p_ref.shape[3]
+    place = ring_place(me, n)
+    rows = x_ref.shape[0]
+    sub = rows // pieces
+    share = rows // heads
+    columns = w_ref.shape[1]
+    half = n // 2
+    ways = (1, -1)
+    beside = [ring_index(place + way, n) for way in ways]
+    weights = pltpu.make_async_copy(w_hbm, w_ref, w_sem.at[0])
+    weights.start()
     barrier = pltpu.get_barrier_semaphore()
     for k in range(1, heads):
         pl.semaphore_signal(barrier, inc=1, device_id={"head": lax.rem(mine + k, heads)}, device_id_type=MESH)
     for k in range(1, n):
         pl.semaphore_signal(barrier, inc=1, device_id={"seq": lax.rem(me + k, n)}, device_id_type=MESH)
     pl.semaphore_wait(barrier, heads + n - 2)
-    first = []
-    for k in range(1, heads):
+
+    def owner_of(way, step):
+        return ring_index(place - ways[way] * step, n)
+
+    def copy(way, step, piece, first):
+        there = (owner_of(way, step), pl.ds(piece * sub, sub))
+        return pltpu.make_async_remote_copy(
+            src_ref=x_ref.at[pl.ds(piece * sub, sub)] if first else blocks.at[there],
+            dst_ref=blocks.at[there],
+            send_sem=send_sem.at[way, step, piece],
+            recv_sem=recv_sem.at[way, step, piece],
+            device_id={"seq": beside[way]},
+            device_id_type=MESH,
+        )
+
+    def to_head(i, k):
         to = lax.rem(mine + k, heads)
-        first.append(
-            pltpu.make_async_remote_copy(
-                src_ref=p_ref.at[to],
-                dst_ref=got.at[k],
-                send_sem=hsend.at[k],
-                recv_sem=hrecv.at[k],
-                device_id={"head": to},
-                device_id_type=MESH,
-            )
+        return pltpu.make_async_remote_copy(
+            src_ref=split.at[i, to],
+            dst_ref=got.at[i, k],
+            send_sem=hsend.at[i, k],
+            recv_sem=hrecv.at[i, k],
+            device_id={"head": to},
+            device_id_type=MESH,
         )
-    for one in first:
-        one.start()
-    for one in first:
-        one.wait()
-
-    def add(i, carry):
-        total = p_ref[mine, i].astype(jnp.float32)
+
+    def to_row(k):
+        to = lax.rem(me + k, n)
+        return pltpu.make_async_remote_copy(
+            src_ref=summed.at[to],
+            dst_ref=landed.at[me],
+            send_sem=fsend.at[k],
+            recv_sem=frecv.at[k],
+            device_id={"seq": to},
+            device_id_type=MESH,
+        )
+
+    def multiply(i, piece, value):
+        product = jnp.dot(value, w_ref[...], preferred_element_type=jnp.float32).astype(jnp.bfloat16)
+        for s in range(sub // share):
+            split[i, piece * (sub // share) + s] = product[s * share : (s + 1) * share]
+
+    def give(i):
         for k in range(1, heads):
-            total = total + got[k, i].astype(jnp.float32)
-        summed[i] = total.astype(jnp.bfloat16)
+            to_head(i, k).start()
+
+    def total_of(i):
+        total = split[i, mine].astype(jnp.float32)
+        for k in range(1, heads):
+            to_head(i, k).wait_recv()
+            total = total + got[i, k].astype(jnp.float32)
+        return total.astype(jnp.bfloat16)
+
+    def settle(i):
+        summed[i] = total_of(i)
+        to_row(lax.rem(i - me + n, n)).start()
+
+    for spot in range(pieces):
+        for way in range(2):
+            copy(way, 0, spot if way == 0 else pieces - 1 - spot, True).start()
+    weights.wait()
+    for piece in range(pieces):
+        multiply(me, piece, x_ref[piece * sub : (piece + 1) * sub])
+    give(me)
+
+    def take(way, step, piece, forward):
+        copy(way, step - 1, piece, False).wait_recv()
+        if forward:
+            copy(way, step, piece, False).start()
+        i = owner_of(way, step)
+        multiply(i, piece, blocks[i, piece * sub : (piece + 1) * sub])
+
+    def one_step(step, last):
+        for spot in range(pieces):
+            for way in range(2):
+                take(way, step, spot if way == 0 else pieces - 1 - spot, not last or spot < pieces // 2)
+        for way in range(2):
+            give(owner_of(way, step))
+
+    one_step(1, half == 2)
+    landed[me] = total_of(me)
+
+    def middle(step, carry):
+        one_step(step, False)
+        for way in range(2):
+            settle(owner_of(way, step - 1))
         return carry
 
-    lax.fori_loop(0, n, add, 0)
-    second = []
+    lax.fori_loop(2, half - 1, middle, 0)
+    if half > 2:
+        one_step(half - 1, True)
+        for way in range(2):
+            settle(owner_of(way, half - 2))
+    for spot in range(pieces // 2):
+        for way in range(2):
+            take(way, half, spot if way == 0 else pieces - 1 - spot, False)
+    give(owner_of(0, half))
+    for way in range(2):
+        settle(owner_of(way, half - 1))
+    settle(owner_of(0, half))
+
+    for spot in range(pieces):
+        for way in range(2):
+            copy(way, 0, spot if way == 0 else pieces - 1 - spot, True).wait_send()
+
+    def drain(step, carry):
+        for piece in range(pieces):
+            for way in range(2):
+                copy(way, step, piece, False).wait_send()
+        return carry
+
+    lax.fori_loop(1, half - 1, drain, 0)
+    if half > 1:
+        for spot in range(pieces // 2):
+            for way in range(2):
+                copy(way, half - 1, spot if way == 0 else pieces - 1 - spot, False).wait_send()
+
+    def drain_heads(i, carry):
+        for k in range(1, heads):
+            to_head(i, k).wait_send()
+        return carry
+
+    lax.fori_loop(0, n, drain_heads, 0)
     for k in range(1, n):
-        to = lax.rem(me + k, n)
-        second.append(
-            pltpu.make_async_remote_copy(
-                src_ref=summed.at[to],
-                dst_ref=landed.at[me],
-                send_sem=send_sem.at[k],
-                recv_sem=recv_sem.at[k],
-                device_id={"seq": to},
-                device_id_type=MESH,
-            )
-        )
-    for one in second:
-        one.start()
-    landed[me] = summed[me]
-    for one in second:
-        one.wait()
+        to_row(k).wait()
     for i in range(n):
         out_ref[:, i * columns : (i + 1) * columns] = landed[i]
 
 
-def finished(split):
-    heads, n, share, columns = split.shape
+def projected(x, weight, n, heads, pieces):
+    rows, width = x.shape
+    columns = weight.shape[1]
+    share = rows // heads
     vmem = pl.BlockSpec(memory_space=pltpu.VMEM)
+    dma = pltpu.SemaphoreType.DMA
     return pl.pallas_call(
-        functools.partial(finish_kernel, n, heads),
-        in_specs=[vmem],
+        functools.partial(project_kernel, n, heads, pieces),
+        in_specs=[vmem, pl.BlockSpec(memory_space=pl.ANY)],
         out_specs=vmem,
-        out_shape=jax.ShapeDtypeStruct((share, n * columns), split.dtype),
+        out_shape=jax.ShapeDtypeStruct((share, n * columns), x.dtype),
         scratch_shapes=[
-            pltpu.VMEM(split.shape, split.dtype),
-            pltpu.VMEM((n, share, columns), split.dtype),
-            pltpu.VMEM((n, share, columns), split.dtype),
-            pltpu.SemaphoreType.DMA((heads,)),
-            pltpu.SemaphoreType.DMA((heads,)),
-            pltpu.SemaphoreType.DMA((n,)),
-            pltpu.SemaphoreType.DMA((n,)),
+            pltpu.VMEM(weight.shape, weight.dtype),
+            pltpu.VMEM((n, rows, width), x.dtype),
+            pltpu.VMEM((n, heads, share, columns), x.dtype),
+            pltpu.VMEM((n, heads, share, columns), x.dtype),
+            pltpu.VMEM((n, share, columns), x.dtype),
+            pltpu.VMEM((n, share, columns), x.dtype),
+            dma((1,)),
+            dma((2, n // 2, pieces)),
+            dma((2, n // 2, pieces)),
+            dma((n, heads)),
+            dma((n, heads)),
+            dma((n,)),
+            dma((n,)),
         ],
         compiler_params=pltpu.CompilerParams(
-            collective_id=3, has_side_effects=True, vmem_limit_bytes=50 << 20
+            collective_id=2, has_side_effects=True, vmem_limit_bytes=56 << 20
         ),
-    )(split)
+    )(x, weight)
 
 
 def body(
@@ -492,12 +611,7 @@
             collective_id=1, has_side_effects=True, vmem_limit_bytes=50 << 20
         ),
     )(parts, lse)
-    (all_attended,) = gathered(attended, n, 2, 2)
-    partial_value = jnp.dot(all_attended, out_weight, preferred_element_type=jnp.float32).astype(jnp.bfloat16)
-    columns = out_weight.shape[1]
-    share = local_rows // head_count
-    split = partial_value.reshape(n, head_count, share, columns).transpose(1, 0, 2, 3)
-    return finished(split)
+    return projected(attended, out_weight, n, head_count, 2)
 
 
 def solution(mesh):

time: 208 us -> 184 us (0.88)
  the two profiles are of different devices: /device:TPU:13 before, /device:TPU:3 now
where the time goes in v1:
time: 184 us
  Pallas kernels  169 us (92%)
  local copies, waits for them, and re-layouts  14.6 us (8%)
    pallas_call x1, Pallas kernels, projected(): pl.pallas_call(functools.partial(project_kernel, n, heads, pieces), in_sp...  59.8 us
    pallas_call x1, Pallas kernels, body(): pl.pallas_call(functools.partial(reduce_kernel, n), in_specs=[pl.BlockSpe...  49.5 us
    pallas_call x1, Pallas kernels, gathered(): pl.pallas_call(functools.partial(gather_kernel, n, pieces, with_table), i...  47.1 us
    unnamed x19, local copies, waits for them, and re-layouts  13.5 us
    pallas_call x1, Pallas kernels, body(): pl.pallas_call(functools.partial(part_kernel, local_blocks, store_blocks)...  12.6 us

profile of v1, /device:TPU:3, one launch (start us, length us, event | category | flops | bytes accessed | tf_op | source)
XLA Modules:
  0.0 184.4 jit_solution(12527315469972076676)
XLA Ops:
  0.0 0.7 copy.11
  0.7 0.8 pad_add_fusion
  1.5 0.0 copy-start.5
  1.5 1.0 copy-done.5
  2.5 47.1 %shard_map.91 = (bf16[2048,1024]{1,0:T(8,128)(2,1)}, s32[8,8,128]{2,1,0:T(8,128)S(1)}) custom-call(bf16[256,1024]{1,0:T(8,128)(2,1)S(1)} %copy-done.5, s32[8,128]{1,0:T(8,128)S(1)} %pad.4.refs_1_), custom_call_target="tpu_custom_call" | custom-call | tf_op jit(solution)/shard_map/pallas_call | solution.py:221
  49.7 0.3 slice_reduce_fusion
  50.0 0.1 reshape_squeeze.3.count_ref
  50.0 0.0 copy-start.1
  50.0 2.2 %copy-done.1 = bf16[2048,1024]{1,0:T(8,128)(2,1)S(1)} copy-done((bf16[2048,1024]{1,0:T(8,128)(2,1)S(1)}, bf16[2048,1024]{1,0:T(8,128)(2,1)}, u32[]{:S(2)}) %copy-start.1) | copy-done | bytes 4194328
  52.2 0.0 copy-start.3
  52.2 1.6 copy-done.3
  53.8 0.0 copy-start.4
  53.8 1.6 copy-done.4
  55.4 0.0 copy-start.6
  55.4 0.9 copy-done.6
  56.3 0.0 copy-start.7
  56.3 0.9 copy-done.7
  57.2 0.0 copy-start.8
  57.2 0.7 copy-done.8
  57.9 12.6 %shard_map.92 = (bf16[16,2,128,512]{3,2,1,0:T(8,128)(2,1)S(1)}, f32[16,2,8,128]{3,2,1,0:T(8,128)S(1)}) custom-call(s32[256]{0:T(256)S(1)} %copy-done.8, s32[16,64]{1,0:T(8,128)S(1)} %bitcast.2, s32[16]{0:T(128)S(1)} %reshape_squeeze.3.count_ref, bf16[2048,1024]{1,0:T(8,128)(2,1)S(1)} %copy-done.1, bf16[256,256]{1,0:T(8,128)(2,1)S(1)} %copy-done.6, ...), custom_call_target="tpu_custom_call" | custom-call | flops 2000000000 | bytes 12582912 | tf_op jit(solution)/shard_map/pallas_call | solution.py:572
  70.5 0.0 copy-start
  70.5 1.9 %copy-done = bf16[16,2,128,512]{3,2,1,0:T(8,128)(2,1)} copy-done((bf16[16,2,128,512]{3,2,1,0:T(8,128)(2,1)}, bf16[16,2,128,512]{3,2,1,0:T(8,128)(2,1)S(1)}, u32[]{:S(2)}) %copy-start) | copy-done | bytes 4194328
  72.4 49.5 %shard_map.93.x_ref = bf16[256,1024]{1,0:T(8,128)(2,1)S(1)} custom-call(bf16[16,2,128,512]{3,2,1,0:T(8,128)(2,1)} %copy-done, f32[16,2,8,128]{3,2,1,0:T(8,128)S(1)} %get-tuple-element.12.lse_ref), custom_call_target="tpu_custom_call" | custom-call | tf_op jit(solution)/shard_map/pallas_call | solution.py:595
  121.9 0.0 copy-start.2
  122.0 0.8 copy-done.2
  122.7 59.8 %shard_map.94 = bf16[64,4096]{1,0:T(8,128)(2,1)} custom-call(bf16[256,1024]{1,0:T(8,128)(2,1)} %copy-done.2, bf16[1024,512]{1,0:T(8,128)(2,1)} %w_hbm.1), custom_call_target="tpu_custom_call" | custom-call | tf_op jit(solution)/shard_map/pallas_call | solution.py:516
  182.6 1.9 %copy.13 = bf16[64,4096]{1,0:T(8,128)(2,1)} copy(bf16[64,4096]{1,0:T(8,128)(2,1)} %shard_map.94) | data formatting | bytes 1048576
  (2 shorter events, 0.0 us)
Async XLA Ops:
  1.5 1.0 copy-start.5
  50.0 2.2 %copy-start.1 = (bf16[2048,1024]{1,0:T(8,128)(2,1)S(1)}, bf16[2048,1024]{1,0:T(8,128)(2,1)}, u32[]{:S(2)}) copy-start(bf16[2048,1024]{1,0:T(8,128)(2,1)} %get-tuple-element.10.q_ref) | copy-start | bytes 12582916
  52.2 1.6 copy-start.3
  53.8 1.6 copy-start.4
  55.4 0.9 copy-start.6
  56.3 0.9 copy-start.7
  57.2 0.7 copy-start.8
  70.5 1.9 %copy-start = (bf16[16,2,128,512]{3,2,1,0:T(8,128)(2,1)}, bf16[16,2,128,512]{3,2,1,0:T(8,128)(2,1)S(1)}, u32[]{:S(2)}) copy-start(bf16[16,2,128,512]{3,2,1,0:T(8,128)(2,1)S(1)} %get-tuple-element.11.o_ref) | copy-start | bytes 12582916
  121.9 0.8 copy-start.2

commit v2 on v1

--- a/solution.py
+++ b/solution.py
@@ -13,12 +13,14 @@
 BLK = 128
 NEG = -1e30
 STAT = 8
+LOG2E = 1.4426950408889634
 MESH = pl.DeviceIdType.MESH
 
 
 def part_kernel(
     local_blocks,
     store_blocks,
+    small,
     slot_ref,
     near_ref,
     count_ref,
@@ -39,52 +41,57 @@
     per_group = H // KVH
     kv_here = k_ref.shape[1] // DH
     rows = per_group * BLK
-    scaling = DH ** (-0.5)
+    scaling = DH ** (-0.5) * LOG2E
+    here = block if small else 0
+    owner, inner = block // local_blocks, lax.rem(block, local_blocks)
+    first_row = pl.multiple_of(block * BLK, BLK) if small else 0
 
     def scan_entry(e, found):
-        slot = slot_ref[near_ref[block, e]]
+        slot = slot_ref[near_ref[owner, inner, e]]
         list_ref[found] = lax.rem(slot, store_blocks)
         return found + (slot // store_blocks == me).astype(jnp.int32)
 
-    found = lax.fori_loop(0, count_ref[block], scan_entry, jnp.int32(0))
+    found = lax.fori_loop(0, count_ref[owner, 0, inner], scan_entry, jnp.int32(0))
     home = block // local_blocks == me
 
     @pl.when(jnp.logical_and(found == 0, jnp.logical_not(home)))
     def _():
-        o_ref[...] = jnp.zeros_like(o_ref)
-        lse_ref[...] = jnp.full_like(lse_ref, NEG)
+        o_ref[here] = jnp.zeros(o_ref.shape[1:], o_ref.dtype)
+        lse_ref[here] = jnp.full(lse_ref.shape[1:], NEG, lse_ref.dtype)
 
     @pl.when(jnp.logical_or(found > 0, home))
     def _():
-        def group_queries(g):
-            return jnp.concatenate(
-                [q_ref[:, (g * per_group + r) * DH : (g * per_group + r + 1) * DH] for r in range(per_group)],
+        def scores_of(g, keys):
+            asked = jnp.concatenate(
+                [
+                    q_ref[pl.ds(first_row, BLK), (g * per_group + r) * DH : (g * per_group + r + 1) * DH]
+                    for r in range(per_group)
+                ],
                 axis=0,
             )
-
-        def scores_of(g, keys):
             return (
-                lax.dot_general(
-                    group_queries(g), keys, (((1,), (1,)), ((), ())), preferred_element_type=jnp.float32
-                )
+                lax.dot_general(keys, asked, (((1,), (1,)), ((), ())), preferred_element_type=jnp.float32)
                 * scaling
+            )
+
+        def weighed(values, p):
+            return lax.dot_general(
+                values, p.astype(jnp.bfloat16), (((0,), (0,)), ((), ())), preferred_element_type=jnp.float32
             )
 
         @pl.when(home)
         def _():
             start = pl.multiple_of(lax.rem(block, local_blocks) * BLK, BLK)
-            position = lax.rem(lax.broadcasted_iota(jnp.int32, (rows, BLK), 0), BLK)
-            causal = position >= lax.broadcasted_iota(jnp.int32, (rows, BLK), 1)
+            position = lax.rem(lax.broadcasted_iota(jnp.int32, (BLK, rows), 1), BLK)
+            causal = position >= lax.broadcasted_iota(jnp.int32, (BLK, rows), 0)
             for g in range(kv_here):
                 cols = slice(g * DH, (g + 1) * DH)
                 s = jnp.where(causal, scores_of(g, sk_ref[pl.ds(start, BLK), cols]), NEG)
-                m = jnp.max(s, axis=-1, keepdims=True)
-                p = jnp.exp(s - m)
-                max_ref[g] = jnp.broadcast_to(m, (rows, BLK))
-                sum_ref[g] = jnp.broadcast_to(jnp.sum(p, axis=-1, keepdims=True), (rows, BLK))
-                acc_ref[g] = jnp.dot(
-                    p.astype(jnp.bfloat16), sv_ref[pl.ds(start, BLK), cols], preferred_element_type=jnp.float32
-                )
+                m = jnp.max(s, axis=0, keepdims=True)
+                p = jnp.exp2(s - m)
+                max_ref[g : g + 1] = m
+                sum_ref[g : g + 1] = jnp.sum(p, axis=0, keepdims=True)
+                acc_ref[g] = weighed(sv_ref[pl.ds(start, BLK), cols], p)
 
         @pl.when(jnp.logical_not(home))
         def _():
@@ -98,26 +105,35 @@
             for g in range(kv_here):
                 cols = slice(g * DH, (g + 1) * DH)
                 s = scores_of(g, k_ref[pl.ds(start, BLK), cols])
-                old = max_ref[g]
-                new = jnp.maximum(old, jnp.max(s, axis=-1, keepdims=True))
-                p = jnp.exp(s - new)
-                shrink = jnp.exp(old - new)
-                max_ref[g] = new
-                sum_ref[g] = sum_ref[g] * shrink + jnp.sum(p, axis=-1, keepdims=True)
-                acc_ref[g] = acc_ref[g] * shrink + jnp.dot(
-                    p.astype(jnp.bfloat16), v_ref[pl.ds(start, BLK), cols], preferred_element_type=jnp.float32
-                )
-
-        lane = lax.broadcasted_iota(jnp.int32, (BLK, BLK), 1)
+                old = max_ref[g : g + 1]
+                new = jnp.maximum(old, jnp.max(s, axis=0, keepdims=True))
+                p = jnp.exp2(s - new)
+                shrink = jnp.exp2(old - new)
+                max_ref[g : g + 1] = new
+                sum_ref[g : g + 1] = sum_ref[g : g + 1] * shrink + jnp.sum(p, axis=0, keepdims=True)
+                acc_ref[g] = acc_ref[g] * shrink + weighed(v_ref[pl.ds(start, BLK), cols], p)
+
         for g in range(kv_here):
-            total = sum_ref[g]
-            normal = (acc_ref[g] / total).astype(jnp.bfloat16)
-            lse = max_ref[g] + jnp.log(total)
-            tile = jnp.full((BLK, BLK), NEG, jnp.float32)
-            for r in range(per_group):
-                o_ref[0, g, :, r * DH : (r + 1) * DH] = normal[r * BLK : (r + 1) * BLK]
-                tile = jnp.where(lane == r, lse[r * BLK : (r + 1) * BLK], tile)
-            lse_ref[0, g] = jnp.transpose(tile)[:STAT]
+            total = sum_ref[g : g + 1]
+            lse = max_ref[g : g + 1] + jnp.log2(total)
+            o_ref[here, g] = (acc_ref[g] * (1.0 / total)).astype(jnp.bfloat16)
+            for r in range(STAT):
+                at = (r % per_group) * BLK
+                lse_ref[here, g, r : r + 1] = lse[:, at : at + BLK]
+
+
+def grant(*arrays):
+    size = 0
+    for shape, dtype in arrays:
+        cells = 1
+        for d in shape:
+            cells = cells * d
+        size += cells * jnp.dtype(dtype).itemsize
+    return min(size + (4 << 20), 60 << 20)
+
+
+def long_cost():
+    return pl.CostEstimate(flops=200_000_000_000, bytes_accessed=1 << 20, transcendentals=0)
 
 
 def ring_place(index, n):
@@ -132,11 +148,21 @@
     return (1 - far) * (2 * place) + far * (2 * (n - 1 - place) + 1)
 
 
-def gather_kernel(n, pieces, with_table, *refs):
-    if with_table:
-        x_ref, table_ref, out_ref, tables_ref, own_sem, send_sem, recv_sem, tsend_sem, trecv_sem = refs
-    else:
-        x_ref, out_ref, own_sem, send_sem, recv_sem = refs
+def gather_kernel(
+    n,
+    pieces,
+    x_ref,
+    near_ref,
+    count_ref,
+    out_ref,
+    nears_ref,
+    counts_ref,
+    own_sem,
+    send_sem,
+    recv_sem,
+    tsend_sem,
+    trecv_sem,
+):
     me = lax.axis_index("seq")
     place = ring_place(me, n)
     rows = x_ref.shape[0]
@@ -144,23 +170,30 @@
     half = n // 2
     ways = (1, -1)
     beside = [ring_index(place + way, n) for way in ways]
+    own = [
+        pltpu.make_async_copy(source, target, own_sem.at[i])
+        for i, (source, target) in enumerate(
+            (
+                (x_ref, out_ref.at[pl.ds(pl.multiple_of(me * rows, rows), rows)]),
+                (near_ref, nears_ref.at[me]),
+                (count_ref, counts_ref.at[me]),
+            )
+        )
+    ]
+    for one in own:
+        one.start()
     barrier = pltpu.get_barrier_semaphore()
-    if with_table:
-        for k in range(1, n):
-            pl.semaphore_signal(barrier, inc=1, device_id={"seq": lax.rem(me + k, n)}, device_id_type=MESH)
-    else:
-        for other in beside:
-            pl.semaphore_signal(barrier, inc=1, device_id={"seq": other}, device_id_type=MESH)
-    own = pltpu.make_async_copy(x_ref, out_ref.at[pl.ds(pl.multiple_of(me * rows, rows), rows)], own_sem.at[0])
-    own.start()
-    pl.semaphore_wait(barrier, n - 1 if with_table else 2)
+    for k in range(1, n):
+        pl.semaphore_signal(barrier, inc=1, device_id={"seq": lax.rem(me + k, n)}, device_id_type=MESH)
+    for one in own:
+        one.wait()
+    pl.semaphore_wait(barrier, n - 1)
 
     def copy(way, step, piece):
         owner = ring_index(place - ways[way] * step, n)
         there = pl.ds(pl.multiple_of(owner * rows + piece * sub, sub), sub)
-        source = x_ref.at[pl.ds(piece * sub, sub)] if step == 0 else out_ref.at[there]
         return pltpu.make_async_remote_copy(
-            src_ref=source,
+            src_ref=out_ref.at[there],
             dst_ref=out_ref.at[there],
             send_sem=send_sem.at[way, step, piece],
             recv_sem=recv_sem.at[way, step, piece],
@@ -168,29 +201,32 @@
             device_id_type=MESH,
         )
 
+    started = []
+    for spot in range(pieces):
+        for way in range(2):
+            one = copy(way, 0, spot if way == 0 else pieces - 1 - spot)
+            one.start()
+            started.append(one)
     table_copies = []
-    if with_table:
-        tables_ref[pl.ds(me, 1)] = table_ref[...][None]
+    for t, target in enumerate((nears_ref, counts_ref)):
         for k in range(1, n):
             table_copies.append(
                 pltpu.make_async_remote_copy(
-                    src_ref=table_ref,
-                    dst_ref=tables_ref.at[me],
-                    send_sem=tsend_sem.at[k],
-                    recv_sem=trecv_sem.at[k],
+                    src_ref=target.at[me],
+                    dst_ref=target.at[me],
+                    send_sem=tsend_sem.at[t, k],
+                    recv_sem=trecv_sem.at[t, k],
                     device_id={"seq": lax.rem(me + k, n)},
                     device_id_type=MESH,
                 )
             )
-        for one in table_copies:
-            one.start()
-    started = []
-    for step in range(half):
+    for one in table_copies:
+        one.start()
+    for step in range(1, half):
         for spot in range(pieces):
             for way in range(2):
                 piece = spot if way == 0 else pieces - 1 - spot
-                if step > 0:
-                    copy(way, step - 1, piece).wait_recv()
+                copy(way, step - 1, piece).wait_recv()
                 if step < half - 1 or spot < pieces // 2:
                     one = copy(way, step, piece)
                     one.start()
@@ -202,44 +238,49 @@
         one.wait_send()
     for one in table_copies:
         one.wait()
-    own.wait()
-
-
-def gathered(x, n, pieces, number, table=None):
+
+
+def gathered(x, near, count, n, pieces):
     rows, width = x.shape
-    with_table = table is not None
     vmem = pl.BlockSpec(memory_space=pltpu.VMEM)
-    out_shape = [jax.ShapeDtypeStruct((n * rows, width), x.dtype)]
-    scratch = [
-        pltpu.SemaphoreType.DMA((1,)),
-        pltpu.SemaphoreType.DMA((2, n // 2, pieces)),
-        pltpu.SemaphoreType.DMA((2, n // 2, pieces)),
-    ]
-    if with_table:
-        out_shape.append(jax.ShapeDtypeStruct((n,) + table.shape, table.dtype))
-        scratch += [pltpu.SemaphoreType.DMA((n,)), pltpu.SemaphoreType.DMA((n,))]
+    size = n * rows * width * x.dtype.itemsize
+    kind = pltpu.VMEM if size <= 8 << 20 else jax.ShapeDtypeStruct
     return pl.pallas_call(
-        functools.partial(gather_kernel, n, pieces, with_table),
-        in_specs=[vmem] * (1 + with_table),
-        out_specs=[vmem] * (1 + with_table),
-        out_shape=out_shape,
-        scratch_shapes=scratch,
+        functools.partial(gather_kernel, n, pieces),
+        in_specs=[pl.BlockSpec(memory_space=pltpu.HBM)] * 3,
+        out_specs=[vmem] * 3,
+        out_shape=[
+            kind((n * rows, width), x.dtype),
+            jax.ShapeDtypeStruct((n,) + near.shape, near.dtype),
+            jax.ShapeDtypeStruct((n,) + count.shape, count.dtype),
+        ],
+        scratch_shapes=[
+            pltpu.SemaphoreType.DMA((3,)),
+            pltpu.SemaphoreType.DMA((2, n // 2, pieces)),
+            pltpu.SemaphoreType.DMA((2, n // 2, pieces)),
+            pltpu.SemaphoreType.DMA((2, n)),
+            pltpu.SemaphoreType.DMA((2, n)),
+        ],
         compiler_params=pltpu.CompilerParams(
-            collective_id=number, has_side_effects=True, vmem_limit_bytes=50 << 20
+            collective_id=0,
+            has_side_effects=True,
+            vmem_limit_bytes=grant((x.shape, x.dtype), ((n * rows, width), x.dtype)),
         ),
-    )(*([x, table] if with_table else [x]))
+        cost_estimate=long_cost(),
+    )(x, near, count)
 
 
 def merge(lse_a, lse_b):
     top = jnp.maximum(lse_a, lse_b)
-    a = jnp.exp(lse_a - top)
-    b = jnp.exp(lse_b - top)
+    a = jnp.exp2(lse_a - top)
+    b = jnp.exp2(lse_b - top)
     total = a + b
-    both = jnp.concatenate([a / total, b / total, jnp.zeros((BLK - 2 * STAT, BLK), jnp.float32)], axis=0)
-    return jnp.transpose(both), top + jnp.log(total)
-
-
-def reduce_kernel(n, o_ref, lse_ref, out_ref, got, got_lse, own, own_sem, send_sem, recv_sem, lsend_sem, lrecv_sem):
+    return a / total, b / total, top + jnp.log2(total)
+
+
+def reduce_kernel(
+    n, small, o_ref, lse_ref, out_ref, got, got_lse, own, own_sem, send_sem, recv_sem, lsend_sem, lrecv_sem
+):
     me = lax.axis_index("seq")
     place = ring_place(me, n)
     groups, width = got.shape[2], got.shape[4]
@@ -282,21 +323,23 @@
     def merged(way, step, g):
         for one in copies(way, step - 1, g, step - 1):
             one.wait_recv()
-        if g == 0:
+        if g == 0 and not small:
             fetch(way, step).wait()
         at = home(way, step) * 2 + way
-        shares, lse = merge(got_lse[way, step - 1, g], lse_ref[at, g])
+        theirs, ours, lse = merge(got_lse[way, step - 1, g], lse_ref[at, g])
         columns = []
         for r in range(width // DH):
             cols = slice(r * DH, (r + 1) * DH)
+            mine = o_ref[at, g, :, cols] if small else own[way, lax.rem(step, 2), g, :, cols]
             columns.append(
-                got[way, step - 1, g, :, cols].astype(jnp.float32) * shares[:, r : r + 1]
-                + own[way, lax.rem(step, 2), g, :, cols].astype(jnp.float32) * shares[:, STAT + r : STAT + r + 1]
+                got[way, step - 1, g, :, cols].astype(jnp.float32) * theirs[r : r + 1]
+                + mine.astype(jnp.float32) * ours[r : r + 1]
             )
         return columns, lse
 
-    for way in range(2):
-        fetch(way, 1).start()
+    if not small:
+        for way in range(2):
+            fetch(way, 1).start()
     pl.semaphore_wait(barrier, 2)
     for g in range(groups):
         for way in range(2):
@@ -304,15 +347,15 @@
                 one.start()
 
     def one_step(step, carry):
-        for way in range(2):
-            fetch(way, step + 1).start()
+        if not small:
+            for way in range(2):
+                fetch(way, step + 1).start()
         for g in range(groups):
             for way in range(2):
                 columns, lse = merged(way, step, g)
                 got_lse[way, step - 1, g] = lse
                 for r, value in enumerate(columns):
                     got[way, step - 1, g, :, r * DH : (r + 1) * DH] = value.astype(jnp.bfloat16)
-            for way in range(2):
                 for one in copies(way, step, g, step - 1):
                     one.start()
         return carry
@@ -323,7 +366,7 @@
             columns, _ = merged(way, n - 1, g)
             for r, value in enumerate(columns):
                 at = g * width + r * DH
-                out_ref[way * BLK : (way + 1) * BLK, at : at + DH] = value.astype(jnp.bfloat16)
+                out_ref[way * BLK : (way + 1) * BLK, at : at + DH] = jnp.transpose(value).astype(jnp.bfloat16)
     for g in range(groups):
         for way in range(2):
             for one in copies(way, 0, g, None):
@@ -515,7 +558,7 @@
     dma = pltpu.SemaphoreType.DMA
     return pl.pallas_call(
         functools.partial(project_kernel, n, heads, pieces),
-        in_specs=[vmem, pl.BlockSpec(memory_space=pl.ANY)],
+        in_specs=[vmem, pl.BlockSpec(memory_space=pltpu.HBM)],
         out_specs=vmem,
         out_shape=jax.ShapeDtypeStruct((share, n * columns), x.dtype),
         scratch_shapes=[
@@ -534,8 +577,16 @@
             dma((n,)),
         ],
         compiler_params=pltpu.CompilerParams(
-            collective_id=2, has_side_effects=True, vmem_limit_bytes=56 << 20
+            collective_id=2,
+            has_side_effects=True,
+            vmem_limit_bytes=grant(
+                (weight.shape, x.dtype),
+                ((n + 2, rows, width), x.dtype),
+                ((2, n, heads, share, max(columns, BLK)), x.dtype),
+                ((3, n, share, max(columns, BLK)), x.dtype),
+            ),
         ),
+        cost_estimate=long_cost(),
     )(x, weight)
 
 
@@ -559,48 +610,45 @@
     kv_here = store_keys.shape[1] // DH
     group_width = (H // KVH) * DH
     rows = (H // KVH) * BLK
-    table = jnp.concatenate([neighbours, counts[:, None]], axis=1)
-    table = jnp.pad(table, ((0, 8 - local_blocks), (0, 2 * BLK - table.shape[1] - BLK)))
-    all_queries, tables = gathered(queries, n, 2, 0, table)
-    near = tables[:, :local_blocks, :degree].reshape(all_blocks, degree)
-    count = tables[:, :local_blocks, degree].reshape(all_blocks)
+    all_queries, near, count = gathered(queries, neighbours, counts.reshape(1, local_blocks), n, 2)
     smem = pl.BlockSpec(memory_space=pltpu.SMEM)
-
-    def whole(a):
-        return pl.BlockSpec(a.shape, lambda i: (0, 0))
+    small = queries.size * n * queries.dtype.itemsize <= 8 << 20
+    kind = pltpu.VMEM if small else jax.ShapeDtypeStruct
+    q_spec = pl.BlockSpec((BLK, width), lambda i: (i, 0))
+    o_spec = pl.BlockSpec((1, kv_here, BLK, group_width), lambda i: (i, 0, 0, 0))
+    lse_spec = pl.BlockSpec((1, kv_here, STAT, BLK), lambda i: (i, 0, 0, 0))
+    if small:
+        q_spec = o_spec = lse_spec = pl.BlockSpec(memory_space=pltpu.VMEM)
 
     parts, lse = pl.pallas_call(
-        functools.partial(part_kernel, local_blocks, store_blocks),
+        functools.partial(part_kernel, local_blocks, store_blocks, small),
         grid=(all_blocks,),
-        in_specs=[smem, smem, smem, pl.BlockSpec((BLK, width), lambda i: (i, 0))]
-        + [whole(a) for a in (self_keys, self_values, store_keys, store_values)],
-        out_specs=[
-            pl.BlockSpec((1, kv_here, BLK, group_width), lambda i: (i, 0, 0, 0)),
-            pl.BlockSpec((1, kv_here, STAT, BLK), lambda i: (i, 0, 0, 0)),
-        ],
+        in_specs=[smem, smem, smem, q_spec]
+        + [pl.BlockSpec(memory_space=pltpu.VMEM)] * 4,
+        out_specs=[o_spec, lse_spec],
         out_shape=[
-            jax.ShapeDtypeStruct((all_blocks, kv_here, BLK, group_width), jnp.bfloat16),
-            jax.ShapeDtypeStruct((all_blocks, kv_here, STAT, BLK), jnp.float32),
+            kind((all_blocks, kv_here, BLK, group_width), jnp.bfloat16),
+            kind((all_blocks, kv_here, STAT, BLK), jnp.float32),
         ],
         scratch_shapes=[
             pltpu.SMEM((degree + 1,), jnp.int32),
-            pltpu.VMEM((kv_here, rows, DH), jnp.float32),
-            pltpu.VMEM((kv_here, rows, BLK), jnp.float32),
-            pltpu.VMEM((kv_here, rows, BLK), jnp.float32),
+            pltpu.VMEM((kv_here, DH, rows), jnp.float32),
+            pltpu.VMEM((kv_here, rows), jnp.float32),
+            pltpu.VMEM((kv_here, rows), jnp.float32),
         ],
-        compiler_params=pltpu.CompilerParams(vmem_limit_bytes=40 << 20),
+        compiler_params=pltpu.CompilerParams(vmem_limit_bytes=28 << 20),
         cost_estimate=pl.CostEstimate(flops=2_000_000_000, bytes_accessed=12 << 20, transcendentals=4_000_000),
     )(kv_slot, near, count, all_queries, self_keys, self_values, store_keys, store_values)
     dma = pltpu.SemaphoreType.DMA((2, n - 1, kv_here))
     attended = pl.pallas_call(
-        functools.partial(reduce_kernel, n),
-        in_specs=[pl.BlockSpec(memory_space=pl.ANY), pl.BlockSpec(memory_space=pltpu.VMEM)],
+        functools.partial(reduce_kernel, n, small),
+        in_specs=[pl.BlockSpec(memory_space=pltpu.VMEM if small else pl.ANY), pl.BlockSpec(memory_space=pltpu.VMEM)],
         out_specs=pl.BlockSpec(memory_space=pltpu.VMEM),
         out_shape=jax.ShapeDtypeStruct((local_rows, width), jnp.bfloat16),
         scratch_shapes=[
             pltpu.VMEM((2, n - 1, kv_here, BLK, group_width), jnp.bfloat16),
             pltpu.VMEM((2, n - 1, kv_here, STAT, BLK), jnp.float32),
-            pltpu.VMEM((2, 2, kv_here, BLK, group_width), jnp.bfloat16),
+            pltpu.VMEM((2, 2, 1 if small else kv_here, BLK, group_width), jnp.bfloat16),
             pltpu.SemaphoreType.DMA((2, 2)),
             dma,
             dma,
@@ -608,8 +656,16 @@
             dma,
         ],
         compiler_params=pltpu.CompilerParams(
-            collective_id=1, has_side_effects=True, vmem_limit_bytes=50 << 20
+            collective_id=1,
+            has_side_effects=True,
+            vmem_limit_bytes=grant(
+                ((2, n + 1, kv_here, BLK, group_width), jnp.bfloat16),
+                ((2, n - 1, kv_here, STAT, BLK), jnp.float32),
+                (lse.shape, lse.dtype),
+                ((local_rows, width), jnp.bfloat16),
+            ),
         ),
+        cost_estimate=long_cost(),
     )(parts, lse)
     return projected(attended, out_weight, n, head_count, 2)
 

time: 184 us -> 165 us (0.90)
  local copies, waits for them, and re-layouts: 14.6 us -> 3.2 us
  Pallas kernels: 169 us -> 160 us
    unnamed x19, local copies, waits for them, and re-layouts: 13.5 us -> 3.2 us
    pallas_call x3, Pallas kernels: 109 us -> 103 us  [the longest x1 47.7 us: body(): pl.pallas_call(functools.partial(reduce_kernel, n, small), in_specs=[pl.B...]
    pallas_call x1, Pallas kernels: 59.8 us -> 57.5 us  [projected(): pl.pallas_call(functools.partial(project_kernel, n, heads, pieces), in_sp...]
where the time goes in v2:
time: 165 us; the launch traced here: 164 us
  Pallas kernels  160 us (97%)
  local copies, waits for them, and re-layouts  3.2 us (2%)
    pallas_call x1, Pallas kernels, projected(): pl.pallas_call(functools.partial(project_kernel, n, heads, pieces), in_sp...  57.5 us
    pallas_call x1, Pallas kernels, body(): pl.pallas_call(functools.partial(reduce_kernel, n, small), in_specs=[pl.B...  47.7 us
    pallas_call x1, Pallas kernels, gathered(): pl.pallas_call(functools.partial(gather_kernel, n, pieces), in_specs=[pl....  45 us
    pallas_call x1, Pallas kernels, body(): pl.pallas_call(functools.partial(part_kernel, local_blocks, store_blocks,...  10.3 us

profile of v2, /device:TPU:3, one launch (start us, length us, event | category | flops | bytes accessed | tf_op | source)
XLA Modules:
  0.0 163.8 jit_solution(2824799762148433473)
XLA Ops:
  0.0 0.0 copy-start.6
  0.0 1.0 copy-done.6
  1.0 0.0 copy-start.7
  1.0 0.7 copy-done.7
  1.7 0.0 copy-start.8
  1.7 0.7 copy-done.8
  2.4 0.0 copy-start
  2.4 0.0 copy-start.1
  2.4 0.0 copy-start.2
  2.4 0.0 copy-start.3
  2.4 0.0 copy-start.4
  2.4 45.0 %shard_map.91 = (bf16[2048,1024]{1,0:T(8,128)(2,1)S(1)}, s32[8,2,64]{2,1,0:T(2,128)S(1)}, s32[8,1,2]{2,1,0:T(1,128)S(1)}) custom-call(bf16[256,1024]{1,0:T(8,128)(2,1)S(1)} %copy-done.6, s32[2,64]{1,0:T(2,128)S(1)} %copy-done.7, s32[1,2]{1,0:T(1,128)S(1)} %bitcast.1), custom_call_target="tpu_custom_call" | custom-call | flops 199999995904 | bytes 1048576 | tf_op jit(solution)/shard_map/pallas_call | solution.py:248
  47.4 0.0 copy-done
  47.4 0.0 copy-done.1
  47.4 0.0 copy-done.2
  47.4 0.0 copy-done.3
  47.4 0.0 copy-done.4
  47.4 10.3 %shard_map.92 = (bf16[16,2,128,512]{3,2,1,0:T(8,128)(2,1)S(1)}, f32[16,2,8,128]{3,2,1,0:T(8,128)S(1)}) custom-call(s32[256]{0:T(256)S(1)} %copy-done.4, s32[8,2,64]{2,1,0:T(2,128)S(1)} %get-tuple-element.10.near_ref, s32[8,1,2]{2,1,0:T(1,128)S(1)} %get-tuple-element.11.count_ref, bf16[2048,1024]{1,0:T(8,128)(2,1)S(1)} %get-tuple-element.12.q_ref, ...), custom_call_target="tpu_custom_call" | custom-call | flops 2000000000 | bytes 12582912 | tf_op jit(solution)/shard_map/pallas_call | solution.py:623
  57.7 0.0 copy-start.5
  57.7 47.7 %shard_map.93.x_ref = bf16[256,1024]{1,0:T(8,128)(2,1)S(1)} custom-call(bf16[16,2,128,512]{3,2,1,0:T(8,128)(2,1)S(1)} %get-tuple-element.13.o_ref, f32[16,2,8,128]{3,2,1,0:T(8,128)S(1)} %get-tuple-element.14.lse_ref), custom_call_target="tpu_custom_call" | custom-call | flops 199999995904 | bytes 1048576 | tf_op jit(solution)/shard_map/pallas_call | solution.py:643
  105.5 0.0 copy-done.5
  105.5 57.5 %shard_map.94 = bf16[64,4096]{1,0:T(8,128)(2,1)S(1)} custom-call(bf16[256,1024]{1,0:T(8,128)(2,1)S(1)} %shard_map.93.x_ref, bf16[1024,512]{1,0:T(8,128)(2,1)S(1)} %copy-done.5), custom_call_target="tpu_custom_call" | custom-call | flops 199999995904 | bytes 1048576 | tf_op jit(solution)/shard_map/pallas_call | solution.py:559
  163.0 0.8 copy.11
Async XLA Ops:
  0.0 1.0 copy-start.6
  1.0 0.7 copy-start.7
  1.7 0.7 copy-start.8
  2.4 45.0 %copy-start = (bf16[4096,256]{1,0:T(8,128)(2,1)S(1)}, bf16[4096,256]{1,0:T(8,128)(2,1)}, u32[]{:S(2)}) copy-start(bf16[4096,256]{1,0:T(8,128)(2,1)} %k_ref.1) | copy-start | bytes 6291460
  2.4 45.0 %copy-start.1 = (bf16[4096,256]{1,0:T(8,128)(2,1)S(1)}, bf16[4096,256]{1,0:T(8,128)(2,1)}, u32[]{:S(2)}) copy-start(bf16[4096,256]{1,0:T(8,128)(2,1)} %v_ref.1) | copy-start | bytes 6291460
  2.4 45.0 %copy-start.2 = (bf16[256,256]{1,0:T(8,128)(2,1)S(1)}, bf16[256,256]{1,0:T(8,128)(2,1)}, u32[]{:S(2)}) copy-start(bf16[256,256]{1,0:T(8,128)(2,1)} %sk_ref.1) | copy-start | bytes 393220
  2.4 45.0 %copy-start.3 = (bf16[256,256]{1,0:T(8,128)(2,1)S(1)}, bf16[256,256]{1,0:T(8,128)(2,1)}, u32[]{:S(2)}) copy-start(bf16[256,256]{1,0:T(8,128)(2,1)} %sv_ref.1) | copy-start | bytes 393220
  2.4 45.0 %copy-start.4 = (s32[256]{0:T(256)S(1)}, s32[256]{0:T(256)}, u32[]{:S(2)}) copy-start(s32[256]{0:T(256)} %slot_ref.1) | copy-start | bytes 3076
  57.7 47.7 %copy-start.5 = (bf16[1024,512]{1,0:T(8,128)(2,1)S(1)}, bf16[1024,512]{1,0:T(8,128)(2,1)}, u32[]{:S(2)}) copy-start(bf16[1024,512]{1,0:T(8,128)(2,1)} %w_hbm.1) | copy-start | bytes 3145732

commit v3 on v2

--- a/solution.py
+++ b/solution.py
@@ -267,7 +267,7 @@
             vmem_limit_bytes=grant((x.shape, x.dtype), ((n * rows, width), x.dtype)),
         ),
         cost_estimate=long_cost(),
-    )(x, near, count)
+    )(*(pltpu.with_memory_space_constraint(a, pltpu.HBM) for a in (x, near, count)))
 
 
 def merge(lse_a, lse_b):
@@ -385,7 +385,6 @@
 def project_kernel(
     n,
     heads,
-    pieces,
     x_ref,
     w_hbm,
     out_ref,
@@ -396,6 +395,8 @@
     summed,
     landed,
     w_sem,
+    wsend,
+    wrecv,
     send_sem,
     recv_sem,
     hsend,
@@ -405,183 +406,246 @@
 ):
     me = lax.axis_index("seq")
     mine = lax.axis_index("head")
-    place = ring_place(me, n)
-    rows = x_ref.shape[0]
-    sub = rows // pieces
-    share = rows // heads
-    columns = w_ref.shape[1]
-    half = n // 2
+    line = n // 2
+    at, side = me // 2, lax.rem(me, 2)
+    share = x_ref.shape[0] // heads
+    columns = w_ref.shape[2]
     ways = (1, -1)
-    beside = [ring_index(place + way, n) for way in ways]
-    weights = pltpu.make_async_copy(w_hbm, w_ref, w_sem.at[0])
+    early = min(2, line - 1)
+    weights = pltpu.make_async_copy(w_hbm, w_ref.at[0], w_sem.at[0])
     weights.start()
     barrier = pltpu.get_barrier_semaphore()
     for k in range(1, heads):
         pl.semaphore_signal(barrier, inc=1, device_id={"head": lax.rem(mine + k, heads)}, device_id_type=MESH)
-    for k in range(1, n):
-        pl.semaphore_signal(barrier, inc=1, device_id={"seq": lax.rem(me + k, n)}, device_id_type=MESH)
-    pl.semaphore_wait(barrier, heads + n - 2)
-
-    def owner_of(way, step):
-        return ring_index(place - ways[way] * step, n)
+    for k in range(1, line):
+        other = lax.rem(at + k, line) * 2 + side
+        pl.semaphore_signal(barrier, inc=1, device_id={"seq": other}, device_id_type=MESH)
+    partner = at * 2 + 1 - side
+    pl.semaphore_signal(barrier, inc=1, device_id={"seq": partner}, device_id_type=MESH)
+    pl.semaphore_wait(barrier, heads + line - 1)
+
+    def inside(place):
+        return jnp.logical_and(place >= 0, place < line)
 
     def copy(way, step, piece, first):
-        there = (owner_of(way, step), pl.ds(piece * sub, sub))
+        there = (at - ways[way] * step, pl.ds(pl.multiple_of(piece * share, share), share))
         return pltpu.make_async_remote_copy(
-            src_ref=x_ref.at[pl.ds(piece * sub, sub)] if first else blocks.at[there],
+            src_ref=x_ref.at[there[1]] if first else blocks.at[there],
             dst_ref=blocks.at[there],
             send_sem=send_sem.at[way, step, piece],
             recv_sem=recv_sem.at[way, step, piece],
-            device_id={"seq": beside[way]},
+            device_id={"seq": (at + ways[way]) * 2 + side},
             device_id_type=MESH,
         )
 
-    def to_head(i, k):
-        to = lax.rem(mine + k, heads)
+    def leaves(way, step):
+        return jnp.logical_and(inside(at - ways[way] * step), inside(at + ways[way]))
+
+    def to_head(i, j, source, to):
         return pltpu.make_async_remote_copy(
-            src_ref=split.at[i, to],
-            dst_ref=got.at[i, k],
-            send_sem=hsend.at[i, k],
-            recv_sem=hrecv.at[i, k],
+            src_ref=split.at[i, j, to],
+            dst_ref=got.at[i, j, source],
+            send_sem=hsend.at[i, j, to],
+            recv_sem=hrecv.at[i, j, source],
             device_id={"head": to},
             device_id_type=MESH,
         )
 
-    def to_row(k):
-        to = lax.rem(me + k, n)
+    def to_row(i, j, source):
+        owner = source * 2 + (side if j == 0 else 1 - side)
         return pltpu.make_async_remote_copy(
-            src_ref=summed.at[to],
-            dst_ref=landed.at[me],
-            send_sem=fsend.at[k],
-            recv_sem=frecv.at[k],
-            device_id={"seq": to},
+            src_ref=summed.at[i, j],
+            dst_ref=landed.at[owner],
+            send_sem=fsend.at[i, j],
+            recv_sem=frecv.at[source, j],
+            device_id={"seq": i * 2 + side},
             device_id_type=MESH,
         )
 
-    def multiply(i, piece, value):
-        product = jnp.dot(value, w_ref[...], preferred_element_type=jnp.float32).astype(jnp.bfloat16)
-        for s in range(sub // share):
-            split[i, piece * (sub // share) + s] = product[s * share : (s + 1) * share]
-
-    def give(i):
+    def unit(i, c, js, own):
+        rows = pl.ds(pl.multiple_of(c * share, share), share)
+        value = x_ref[rows] if own else blocks[i, rows]
+        for j in js:
+            split[i, j, c] = jnp.dot(value, w_ref[j], preferred_element_type=jnp.float32).astype(jnp.bfloat16)
+
+            @pl.when(mine != c)
+            def _():
+                to_head(i, j, mine, c).start()
+
+    def visit(step, c, js, arriving):
+        for way in range(2):
+            i = at - ways[way] * step
+
+            @pl.when(inside(i))
+            def _():
+                if arriving:
+                    copy(way, step - 1, c, False).wait_recv()
+
+                    @pl.when(inside(at + ways[way]))
+                    def _():
+                        copy(way, step, c, False).start()
+
+                unit(i, c, js, False)
+
+    def total_of(i, j):
+        total = split[i, j, mine].astype(jnp.float32)
         for k in range(1, heads):
-            to_head(i, k).start()
-
-    def total_of(i):
-        total = split[i, mine].astype(jnp.float32)
-        for k in range(1, heads):
-            to_head(i, k).wait_recv()
-            total = total + got[i, k].astype(jnp.float32)
+            source = lax.rem(mine + k, heads)
+            to_head(i, j, source, mine).wait_recv()
+            total = total + got[i, j, source].astype(jnp.float32)
         return total.astype(jnp.bfloat16)
 
-    def settle(i):
-        summed[i] = total_of(i)
-        to_row(lax.rem(i - me + n, n)).start()
-
-    for spot in range(pieces):
-        for way in range(2):
-            copy(way, 0, spot if way == 0 else pieces - 1 - spot, True).start()
+    def settle_own(j):
+        landed[at * 2 + (side if j == 0 else 1 - side)] = total_of(at, j)
+
+    def settle(step, js):
+        for way in range(2):
+            i = at - ways[way] * step
+
+            @pl.when(inside(i))
+            def _():
+                for j in js:
+                    summed[i, j] = total_of(i, j)
+                    to_row(i, j, at).start()
+
+    def each(function):
+        lax.fori_loop(0, heads, lambda c, carry: (function(c), carry)[1], 0)
+
+    def start_own(c):
+        for way in range(2):
+
+            @pl.when(inside(at + ways[way]))
+            def _():
+                copy(way, 0, c, True).start()
+
+    each(start_own)
     weights.wait()
-    for piece in range(pieces):
-        multiply(me, piece, x_ref[piece * sub : (piece + 1) * sub])
-    give(me)
-
-    def take(way, step, piece, forward):
-        copy(way, step - 1, piece, False).wait_recv()
-        if forward:
-            copy(way, step, piece, False).start()
-        i = owner_of(way, step)
-        multiply(i, piece, blocks[i, piece * sub : (piece + 1) * sub])
-
-    def one_step(step, last):
-        for spot in range(pieces):
-            for way in range(2):
-                take(way, step, spot if way == 0 else pieces - 1 - spot, not last or spot < pieces // 2)
-        for way in range(2):
-            give(owner_of(way, step))
-
-    one_step(1, half == 2)
-    landed[me] = total_of(me)
-
-    def middle(step, carry):
-        one_step(step, False)
-        for way in range(2):
-            settle(owner_of(way, step - 1))
+    exchange = pltpu.make_async_remote_copy(
+        src_ref=w_ref.at[0],
+        dst_ref=w_ref.at[1],
+        send_sem=wsend.at[0],
+        recv_sem=wrecv.at[0],
+        device_id={"seq": partner},
+        device_id_type=MESH,
+    )
+    exchange.start()
+    each(lambda c: unit(at, c, (0,), True))
+
+    def first_steps(step, carry):
+        each(lambda c: visit(step, c, (0,), True))
+
+        @pl.when(step == 1)
+        def _():
+            settle_own(0)
+
+        @pl.when(step > 1)
+        def _():
+            settle(step - 1, (0,))
+
         return carry
 
-    lax.fori_loop(2, half - 1, middle, 0)
-    if half > 2:
-        one_step(half - 1, True)
-        for way in range(2):
-            settle(owner_of(way, half - 2))
-    for spot in range(pieces // 2):
-        for way in range(2):
-            take(way, half, spot if way == 0 else pieces - 1 - spot, False)
-    give(owner_of(0, half))
+    lax.fori_loop(1, early + 1, first_steps, 0)
+    exchange.wait()
+    each(lambda c: unit(at, c, (1,), True))
+    lax.fori_loop(1, early + 1, lambda t, carry: (each(lambda c: visit(t, c, (1,), False)), carry)[1], 0)
+    settle(early, (0,))
+
+    def late_step(step, carry):
+        each(lambda c: visit(step, c, (0, 1), True))
+
+        @pl.when(step == early + 1)
+        def _():
+            settle_own(1)
+            lax.fori_loop(1, early + 1, lambda t, inner: (settle(t, (1,)), inner)[1], 0)
+
+        @pl.when(step > early + 1)
+        def _():
+            settle(step - 1, (0, 1))
+
+        return carry
+
+    if line - 1 > early:
+        lax.fori_loop(early + 1, line, late_step, 0)
+        settle(line - 1, (0, 1))
+    else:
+        settle_own(1)
+        lax.fori_loop(1, early + 1, lambda t, inner: (settle(t, (1,)), inner)[1], 0)
+
     for way in range(2):
-        settle(owner_of(way, half - 1))
-    settle(owner_of(0, half))
-
-    for spot in range(pieces):
-        for way in range(2):
-            copy(way, 0, spot if way == 0 else pieces - 1 - spot, True).wait_send()
-
-    def drain(step, carry):
-        for piece in range(pieces):
-            for way in range(2):
-                copy(way, step, piece, False).wait_send()
+        for step in range(2):
+
+            def finish(c):
+                @pl.when(leaves(way, step))
+                def _():
+                    copy(way, step, c, step == 0).wait_send()
+
+            if step == 0:
+                each(finish)
+            else:
+
+                def finish_rest(t, carry):
+                    def one(c):
+                        @pl.when(leaves(way, t))
+                        def _():
+                            copy(way, t, c, False).wait_send()
+
+                    each(one)
+                    return carry
+
+                lax.fori_loop(1, line, finish_rest, 0)
+
+    def drain(i, carry):
+        for j in range(2):
+            for k in range(1, heads):
+                to_head(i, j, mine, lax.rem(mine + k, heads)).wait_send()
+
+            @pl.when(i != at)
+            def _():
+                to_row(i, j, at).wait_send()
+                to_row(at, j, i).wait_recv()
+
         return carry
 
-    lax.fori_loop(1, half - 1, drain, 0)
-    if half > 1:
-        for spot in range(pieces // 2):
-            for way in range(2):
-                copy(way, half - 1, spot if way == 0 else pieces - 1 - spot, False).wait_send()
-
-    def drain_heads(i, carry):
-        for k in range(1, heads):
-            to_head(i, k).wait_send()
-        return carry
-
-    lax.fori_loop(0, n, drain_heads, 0)
-    for k in range(1, n):
-        to_row(k).wait()
+    lax.fori_loop(0, line, drain, 0)
     for i in range(n):
         out_ref[:, i * columns : (i + 1) * columns] = landed[i]
 
 
-def projected(x, weight, n, heads, pieces):
+def projected(x, weight, n, heads):
     rows, width = x.shape
     columns = weight.shape[1]
     share = rows // heads
+    line = n // 2
     vmem = pl.BlockSpec(memory_space=pltpu.VMEM)
     dma = pltpu.SemaphoreType.DMA
     return pl.pallas_call(
-        functools.partial(project_kernel, n, heads, pieces),
-        in_specs=[vmem, pl.BlockSpec(memory_space=pltpu.HBM)],
+        functools.partial(project_kernel, n, heads),
+        in_specs=[vmem, pl.BlockSpec(memory_space=pl.ANY)],
         out_specs=vmem,
         out_shape=jax.ShapeDtypeStruct((share, n * columns), x.dtype),
         scratch_shapes=[
-            pltpu.VMEM(weight.shape, weight.dtype),
-            pltpu.VMEM((n, rows, width), x.dtype),
-            pltpu.VMEM((n, heads, share, columns), x.dtype),
-            pltpu.VMEM((n, heads, share, columns), x.dtype),
-            pltpu.VMEM((n, share, columns), x.dtype),
+            pltpu.VMEM((2,) + weight.shape, weight.dtype),
+            pltpu.VMEM((line, rows, width), x.dtype),
+            pltpu.VMEM((line, 2, heads, share, columns), x.dtype),
+            pltpu.VMEM((line, 2, heads, share, columns), x.dtype),
+            pltpu.VMEM((line, 2, share, columns), x.dtype),
             pltpu.VMEM((n, share, columns), x.dtype),
             dma((1,)),
-            dma((2, n // 2, pieces)),
-            dma((2, n // 2, pieces)),
-            dma((n, heads)),
-            dma((n, heads)),
-            dma((n,)),
-            dma((n,)),
+            dma((1,)),
+            dma((1,)),
+            dma((2, line, heads)),
+            dma((2, line, heads)),
+            dma((line, 2, heads)),
+            dma((line, 2, heads)),
+            dma((line, 2)),
+            dma((line, 2)),
         ],
         compiler_params=pltpu.CompilerParams(
             collective_id=2,
             has_side_effects=True,
             vmem_limit_bytes=grant(
-                (weight.shape, x.dtype),
-                ((n + 2, rows, width), x.dtype),
+                ((2, width, max(columns, BLK)), x.dtype),
+                ((line + 2, rows, width), x.dtype),
                 ((2, n, heads, share, max(columns, BLK)), x.dtype),
                 ((3, n, share, max(columns, BLK)), x.dtype),
             ),
@@ -667,7 +731,7 @@
         ),
         cost_estimate=long_cost(),
     )(parts, lse)
-    return projected(attended, out_weight, n, head_count, 2)
+    return projected(attended, out_weight, n, head_count)
 
 
 def solution(mesh):

time: 165 us -> 156 us (0.945)
  Pallas kernels: 160 us -> 154 us
  local copies, waits for them, and re-layouts: 3.2 us -> 0.82 us
    pallas_call x1, Pallas kernels: 57.5 us -> 51.6 us  [projected(): pl.pallas_call(functools.partial(project_kernel, n, heads), in_specs=[vme...]
    unnamed x19 -> x13, local copies, waits for them, and re-layouts: 3.2 us -> 0.82 us
    pallas_call x1, Pallas kernels: 47.7 us -> 46 us  [body(): pl.pallas_call(functools.partial(reduce_kernel, n, small), in_specs=[pl.B...]
where the time goes in v3:
time: 156 us; the launch traced here: 155 us
  Pallas kernels  154 us (99%)
    pallas_call x1, Pallas kernels, projected(): pl.pallas_call(functools.partial(project_kernel, n, heads), in_specs=[vme...  51.6 us
    pallas_call x1, Pallas kernels, body(): pl.pallas_call(functools.partial(reduce_kernel, n, small), in_specs=[pl.B...  46 us
    pallas_call x1, Pallas kernels, gathered(): pl.pallas_call(functools.partial(gather_kernel, n, pieces), in_specs=[pl....  44.9 us
    pallas_call x1, Pallas kernels, body(): pl.pallas_call(functools.partial(part_kernel, local_blocks, store_blocks,...  11.1 us

profile of v3, /device:TPU:3, one launch (start us, length us, event | category | flops | bytes accessed | tf_op | source)
XLA Modules:
  0.0 154.5 jit_solution(4852367531665451999)
XLA Ops:
  0.0 0.0 copy-start
  0.0 0.0 copy-start.1
  0.0 0.0 copy-start.2
  0.0 0.0 copy-start.3
  0.0 0.0 copy-start.4
  0.0 44.9 %shard_map.91 = (bf16[2048,1024]{1,0:T(8,128)(2,1)S(1)}, s32[8,2,64]{2,1,0:T(2,128)S(1)}, s32[8,1,2]{2,1,0:T(1,128)S(1)}) custom-call(bf16[256,1024]{1,0:T(8,128)(2,1)} %x_ref.1, s32[2,64]{1,0:T(2,128)} %near_ref.1, s32[1,2]{1,0:T(1,128)} %bitcast.1), custom_call_target="tpu_custom_call" | custom-call | flops 199999995904 | bytes 1048576 | tf_op jit(solution)/shard_map/pallas_call | solution.py:248
  44.9 0.0 copy-done
  45.0 0.0 copy-done.1
  45.0 0.0 copy-done.2
  45.0 0.0 copy-done.3
  45.0 0.0 copy-done.4
  45.0 11.1 %shard_map.92 = (bf16[16,2,128,512]{3,2,1,0:T(8,128)(2,1)S(1)}, f32[16,2,8,128]{3,2,1,0:T(8,128)S(1)}) custom-call(s32[256]{0:T(256)S(1)} %copy-done.4, s32[8,2,64]{2,1,0:T(2,128)S(1)} %get-tuple-element.10.near_ref, s32[8,1,2]{2,1,0:T(1,128)S(1)} %get-tuple-element.11.count_ref, bf16[2048,1024]{1,0:T(8,128)(2,1)S(1)} %get-tuple-element.12.q_ref, ...), custom_call_target="tpu_custom_call" | custom-call | flops 2000000000 | bytes 12582912 | tf_op jit(solution)/shard_map/pallas_call | solution.py:687
  56.1 0.0 copy-start.5
  56.1 46.0 %shard_map.93.x_ref = bf16[256,1024]{1,0:T(8,128)(2,1)S(1)} custom-call(bf16[16,2,128,512]{3,2,1,0:T(8,128)(2,1)S(1)} %get-tuple-element.13.o_ref, f32[16,2,8,128]{3,2,1,0:T(8,128)S(1)} %get-tuple-element.14.lse_ref), custom_call_target="tpu_custom_call" | custom-call | flops 199999995904 | bytes 1048576 | tf_op jit(solution)/shard_map/pallas_call | solution.py:707
  102.1 0.0 copy-done.5
  102.1 51.6 %shard_map.94 = bf16[64,4096]{1,0:T(8,128)(2,1)S(1)} custom-call(bf16[256,1024]{1,0:T(8,128)(2,1)S(1)} %shard_map.93.x_ref, bf16[1024,512]{1,0:T(8,128)(2,1)S(1)} %copy-done.5), custom_call_target="tpu_custom_call" | custom-call | flops 199999995904 | bytes 1048576 | tf_op jit(solution)/shard_map/pallas_call | solution.py:621
  153.7 0.8 copy.11
Async XLA Ops:
  0.0 45.0 %copy-start = (bf16[4096,256]{1,0:T(8,128)(2,1)S(1)}, bf16[4096,256]{1,0:T(8,128)(2,1)}, u32[]{:S(2)}) copy-start(bf16[4096,256]{1,0:T(8,128)(2,1)} %k_ref.1) | copy-start | bytes 6291460
  0.0 45.0 %copy-start.1 = (bf16[4096,256]{1,0:T(8,128)(2,1)S(1)}, bf16[4096,256]{1,0:T(8,128)(2,1)}, u32[]{:S(2)}) copy-start(bf16[4096,256]{1,0:T(8,128)(2,1)} %v_ref.1) | copy-start | bytes 6291460
  0.0 45.0 %copy-start.2 = (bf16[256,256]{1,0:T(8,128)(2,1)S(1)}, bf16[256,256]{1,0:T(8,128)(2,1)}, u32[]{:S(2)}) copy-start(bf16[256,256]{1,0:T(8,128)(2,1)} %sk_ref.1) | copy-start | bytes 393220
  0.0 45.0 %copy-start.3 = (bf16[256,256]{1,0:T(8,128)(2,1)S(1)}, bf16[256,256]{1,0:T(8,128)(2,1)}, u32[]{:S(2)}) copy-start(bf16[256,256]{1,0:T(8,128)(2,1)} %sv_ref.1) | copy-start | bytes 393220
  0.0 45.0 %copy-start.4 = (s32[256]{0:T(256)S(1)}, s32[256]{0:T(256)}, u32[]{:S(2)}) copy-start(s32[256]{0:T(256)} %slot_ref.1) | copy-start | bytes 3076
  56.1 46.0 %copy-start.5 = (bf16[1024,512]{1,0:T(8,128)(2,1)S(1)}, bf16[1024,512]{1,0:T(8,128)(2,1)}, u32[]{:S(2)}) copy-start(bf16[1024,512]{1,0:T(8,128)(2,1)} %w_hbm.1) | copy-start | bytes 3145732
